TPU v7x, 32 devices: a whole 2x2x4 slice. The times are simulated.
32 devices in a mesh: dp: 4 (over x, core), pipe: 2 (over y), tensor: 4 (over z).
Axes of the slice: x: 2, y: 2, z: 4, core: 2. Of those that a mesh axis runs over, the one named last changes fastest.
Arguments:
- weights: bfloat16 [2816, 1408], P(('dp', 'pipe', 'tensor')), may hold values from -6 to 6
- first_moment: bfloat16 [2816, 1408], P(('dp', 'pipe', 'tensor')), may hold values from -6 to 6
- second_moment: bfloat16 [2816, 1408], P(('dp', 'pipe', 'tensor')), may hold values from 0.049804688 to 5
- row_weight: float32 [1408], replicated, may hold values from -1 to 1
- col_weight: float32 [1408], replicated, may hold values from 1 to 4
Outputs:
- weight_tiles: bfloat16 [2816, 1408], P(('pipe', 'tensor'))
- first_tiles: bfloat16 [2816, 1408], P(('pipe', 'tensor'))
- second_tiles: bfloat16 [2816, 1408], P(('pipe', 'tensor'))
- checksums: float32 [3, 2, 4, 11], P(None, 'pipe', 'tensor')
All inputs are finite; a program needn't handle non-finite values.
Results may differ from a plain program's by a relative error of at most 0.001.
Values may be sent and summed in bfloat16 or wider, within the bound.
A program may use at most 64 MiB of HBM per device.

v0:
```python
import functools

import jax
import jax.numpy as jnp
from jax import lax
from jax.experimental import pallas as pl
from jax.experimental.pallas import tpu as pltpu
from jax.sharding import PartitionSpec as P

CHECK_COLS = 128
SPLIT = 2
LEAD, START, HOP = 1.5, 2.5, 1.7


def for_sending(array):
    return jax.tree.map(lambda a: a.astype(jnp.bfloat16) if a.dtype == jnp.float32 else a, array)


def column_sums(data, row_part, col_weight, col_blocks):
    row_mixed = jnp.dot(
        row_part[None, :], data.astype(jnp.float32), precision=lax.Precision.HIGHEST
    )[0]
    return jnp.sum((row_mixed * col_weight).reshape(col_blocks, -1), axis=1)


def shards(weights, first_moment, second_moment, row_weight, col_weight):
    dp_count = lax.axis_size("dp")
    pipe_count = lax.axis_size("pipe")
    tensor_count = lax.axis_size("tensor")
    shard_rows, width = weights.shape
    dp_section = dp_count // pipe_count
    tile_shards = dp_count // tensor_count
    piece_cols = width // dp_count
    tile_rows = shard_rows * dp_count
    col_blocks = width // CHECK_COLS
    factor = float(tile_rows * CHECK_COLS) ** (-0.5)
    sources = (weights, first_moment, second_moment)
    exchanged = (
        lax.all_to_all(sources[0], "dp", split_axis=1, concat_axis=0, tiled=True),
        lax.all_to_all(sources[1], "dp", split_axis=1, concat_axis=0, tiled=True),
        lax.all_to_all(sources[2], "dp", split_axis=1, concat_axis=0, tiled=True),
    )
    grouped = tuple(
        (item.reshape(pipe_count, dp_section, shard_rows, piece_cols) for item in exchanged)
    )
    sectioned = jax.tree.map(
        lambda part, own: part.astype(own.dtype),
        lax.all_to_all(for_sending(grouped), "pipe", split_axis=0, concat_axis=2, tiled=True),
        grouped,
    )
    routed = tuple(
        (item.reshape(tensor_count, tile_shards, 1, shard_rows, piece_cols) for item in sectioned)
    )
    arrived = jax.tree.map(
        lambda part, own: part.astype(own.dtype),
        lax.all_to_all(for_sending(routed), "tensor", split_axis=0, concat_axis=2, tiled=True),
        routed,
    )
    flat_pieces = tuple((item.reshape(tile_rows, piece_cols) for item in arrived))
    tiles = jax.tree.map(
        lambda part, own: part.astype(own.dtype),
        lax.all_gather(for_sending(flat_pieces), "dp", axis=1, tiled=True),
        flat_pieces,
    )
    tensor_pos = lax.axis_index("tensor")
    flat_index = (
        lax.axis_index("dp") * pipe_count + lax.axis_index("pipe")
    ) * tensor_count + tensor_pos
    in_section = flat_index % (dp_count * tensor_count)
    section_of = flat_index // (dp_count * tensor_count)
    tile_of = in_section // dp_count
    row_part = lax.dynamic_slice_in_dim(row_weight, in_section * shard_rows, shard_rows)
    partial_value = jnp.stack(
        [column_sums(item, row_part, col_weight, col_blocks) for item in sources]
    )
    section_hit = (jnp.arange(pipe_count) == section_of).astype(jnp.float32)
    tile_hit = (jnp.arange(tensor_count) == tile_of).astype(jnp.float32)
    spread = (
        partial_value[:, None, None, :]
        * section_hit[None, :, None, None]
        * tile_hit[None, None, :, None]
    )
    summed = lax.psum(spread, ("dp", "pipe", "tensor"))
    checks = (
        lax.dynamic_slice(summed, (0, lax.axis_index("pipe"), tensor_pos, 0), (3, 1, 1, col_blocks))
        * factor
    )
    return (tiles[0], tiles[1], tiles[2], checks)


def remote(src, dst, send_sem, recv_sem, where):
    return pltpu.make_async_remote_copy(
        src_ref=src,
        dst_ref=dst,
        send_sem=send_sem,
        recv_sem=recv_sem,
        device_id=where,
        device_id_type=pl.DeviceIdType.MESH,
    )


def route(
    count,
    w_ref,
    m_ref,
    v_ref,
    own,
    src,
    crossed,
    transit,
    load_sem,
    cross_send,
    cross_recv,
    z_send,
    own_recv,
    transit_recv,
    x_send,
    y_send,
    d_send,
):
    dp, y, z = lax.axis_index("dp"), lax.axis_index("pipe"), lax.axis_index("tensor")
    x, core = dp // 2, dp % 2
    active = z // 2 == core
    diag = x == y
    to_x = {"dp": (1 - x) * 2 + core, "pipe": y, "tensor": z}
    to_y = {"dp": dp, "pipe": 1 - y, "tensor": z}
    to_core = {"dp": x * 2 + 1 - core, "pipe": y, "tensor": z}

    def to_z(pos):
        return {"dp": dp, "pipe": y, "tensor": pos}

    ins = (w_ref, m_ref, v_ref)
    loads = [pltpu.make_async_copy(ins[a], src.at[a], load_sem.at[a]) for a in range(3)]
    for load in loads:
        load.start()

    barrier = pltpu.get_barrier_semaphore()
    for where in (to_x, to_y, to_core):
        pl.semaphore_signal(barrier, inc=1, device_id=where, device_id_type=pl.DeviceIdType.MESH)
    for step in range(1, count):
        pl.semaphore_signal(
            barrier,
            inc=1,
            device_id=to_z((z + step) % count),
            device_id_type=pl.DeviceIdType.MESH,
        )
    pl.semaphore_wait(barrier, count + 2)
    for load in loads:
        load.wait()

    width = w_ref.shape[1]
    edges = [width // CHECK_COLS * h // SPLIT * CHECK_COLS for h in range(SPLIT)] + [width]
    cuts = [pl.ds(low, high - low) for low, high in zip(edges, edges[1:])]

    def own_at(a, k, h):
        return own.at[a, k, :, cuts[h]]

    def transit_at(a, k, h):
        return transit.at[a - 1, k, :, cuts[h]]

    def cross(a, h):
        return remote(
            src.at[a, :, cuts[h]],
            crossed.at[:, cuts[h]],
            cross_send.at[h],
            cross_recv.at[h],
            to_y,
        )

    def z_copies(pos, turn, pieces, act):
        for a, h, piece, slot, sem in pieces:
            away = remote(piece, slot, z_send.at[turn, a, h], sem, to_z(pos))
            near = pltpu.make_async_copy(piece, slot, sem)

            @pl.when(pos != z)
            def _():
                if act == "start":
                    away.start()
                else:
                    away.wait_send()

            if act == "start":

                @pl.when(pos == z)
                def _():
                    near.start()

    mine, other = 2 * core + y, 2 * core + 1 - y
    halves = range(len(cuts))

    def to_own(h, arrays, pieces):
        return [(n, h, p, own_at(a, z, h), own_recv.at[a, z, h]) for n, (a, p) in enumerate(zip(arrays, pieces))]

    def to_transit(h, arrays, pieces):
        return [
            (n, h, p, transit_at(a, z, h), transit_recv.at[a - 1, z, h])
            for n, (a, p) in enumerate(zip(arrays, pieces))
        ]

    def source(arrays, h):
        return [src.at[a, :, cuts[h]] for a in arrays]

    def mine_pieces(on_diag, h):
        if on_diag:
            return to_own(h, (0, 1), source((0, 1), h))
        return to_transit(h, (1, 2), source((1, 2), h))

    def other_pieces(on_diag, h):
        place, a = (to_own, 0) if on_diag else (to_transit, 2)
        return place(h, (a,), [crossed.at[:, cuts[h]]])

    for on_diag in (True, False):

        @pl.when(diag == on_diag)
        def _():
            sent = 2 if on_diag else 0
            for h in halves:
                cross(sent, h).start()
            for h in halves:
                z_copies(mine, 0, mine_pieces(on_diag, h), "start")
            for h in halves:
                cross(sent, h).wait_recv()
                z_copies(other, 1, other_pieces(on_diag, h), "start")

    def arrived(a, k, h):
        pltpu.make_async_copy(own_at(a, k, h), own_at(a, k, h), own_recv.at[a, k, h]).wait()

    def passed(a, k, h):
        slot = transit_at(a, k, h)
        pltpu.make_async_copy(slot, slot, transit_recv.at[a - 1, k, h]).wait()

    def own_x(a, k, h):
        slot = own_at(a, k, h)
        return remote(slot, slot, x_send.at[a, k, h], own_recv.at[a, k, h], to_x)

    def transit_x(a, k, h):
        slot = transit_at(a, k, h)
        return remote(slot, slot, x_send.at[a - 1, k, h], transit_recv.at[a - 1, k, h], to_x)

    def transit_y(a, k, h):
        return remote(
            transit_at(a, k, h),
            own_at(a, k, h),
            y_send.at[a - 1, k, h],
            own_recv.at[a, k, h],
            to_y,
        )

    def across(a, k, h):
        slot = own_at(a, k, h)
        return remote(slot, slot, d_send.at[a, k, h], own_recv.at[a, k, h], to_core)

    half = count // 2

    def piece(step):
        if step < half:
            return jnp.where(
                z < half, (z + half - step) % half, half + (z - half + half - step) % half
            )
        return jnp.where(z < half, step, count - 1 - step)

    match = z % 2 == y

    def in_turn(arrays, start, lag):
        turns = [(start + lag, a, 0) for a in arrays]
        for a in arrays:
            turns += [(start + lag + LEAD + len(turns) - len(arrays), a, s) for s in range(1, count)]
        return turns

    def forward(on_diag, on_match):
        direct, passing, late = ((0, 1), (1, 2), (2,)) if on_match else ((0,), (2,), (1, 2))
        start = 0.0 if on_match else START
        hop = HOP
        turns = [(t, "direct", a, s) for t, a, s in in_turn(direct, start, 0.0 if on_diag else hop)]
        turns += [(t, "pass", a, s) for t, a, s in in_turn(passing, start, hop if on_diag else 0.0)]
        turns += [(t, "late", a, s) for t, a, s in in_turn(late, START - start, 2 * hop + 0.1)]
        turns = [(t + 3 * h / SPLIT, way, a, step, h) for t, way, a, step in turns for h in halves]
        for _, way, a, step, h in sorted(turns):
            k = piece(step)
            if way == "pass":
                passed(a, k, h)
                transit_y(a, k, h).start()
                if not on_diag:
                    transit_x(a, k, h).start()
            else:
                arrived(a, k, h)
                if way == "direct" and on_diag:
                    own_x(a, k, h).start()
                across(a, k, h).start()

        @pl.loop(0, count)
        def _(k):
            for h in halves:
                for a in range(3):
                    across(a, k, h).wait_send()
                for a in passing:
                    transit_y(a, k, h).wait_send()
                    if not on_diag:
                        transit_x(a, k, h).wait_send()
                if on_diag:
                    for a in direct:
                        own_x(a, k, h).wait_send()

    for on_diag in (True, False):
        for on_match in (True, False):

            @pl.when(active & (diag == on_diag) & (match == on_match))
            def _():
                forward(on_diag, on_match)

    @pl.when(jnp.logical_not(active))
    def _():
        @pl.loop(0, count)
        def _(k):
            for a in range(3):
                for h in halves:
                    arrived(a, k, h)

    for on_diag in (True, False):

        @pl.when(diag == on_diag)
        def _():
            for h in halves:
                cross(2 if on_diag else 0, h).wait_send()
                z_copies(mine, 0, mine_pieces(on_diag, h), "wait")
                z_copies(other, 1, other_pieces(on_diag, h), "wait")


def finish(count, own, row_ref, col_ref, out0, out1, out2, check_ref, acc, out_sem):
    rows, width = own.shape[2:]
    outs = (out0, out1, out2)
    leaving = [pltpu.make_async_copy(own.at[a], outs[a], out_sem.at[a]) for a in range(3)]
    for copy in leaving:
        copy.start()
    acc[...] = jnp.zeros_like(acc)
    for k in range(count):
        first = (lax.axis_index("tensor") * count + k) * rows
        everyone = jnp.broadcast_to(row_ref[...].reshape(1, width), (8, width))
        part = pltpu.roll(everyone, (width - first) % width, 1)[:, :rows]
        high = part.astype(jnp.bfloat16).astype(jnp.float32)
        middle = (part - high).astype(jnp.bfloat16).astype(jnp.float32)
        low = part - high - middle
        line = lax.broadcasted_iota(jnp.int32, (8, rows), 0)
        terms = jnp.where(
            line == 0, high, jnp.where(line == 1, middle, jnp.where(line == 2, low, 0.0))
        )
        terms = terms.astype(jnp.bfloat16)
        for a in range(3):
            acc[a] += jnp.dot(terms, own[a, k], preferred_element_type=jnp.float32)

    factor = float(rows * count * CHECK_COLS) ** (-0.5)
    blocks = width // CHECK_COLS
    weight = col_ref[...].reshape(1, width)
    for a in range(3):
        mixed = jnp.sum(acc[a], axis=0, keepdims=True) * weight
        lane = lax.broadcasted_iota(jnp.int32, (1, blocks), 1)
        line = jnp.zeros((1, blocks), jnp.float32)
        for e in range(blocks):
            part = jnp.sum(mixed[:, e * CHECK_COLS : (e + 1) * CHECK_COLS], axis=1, keepdims=True)
            line = jnp.where(lane == e, part, line)
        check_ref[a, 0] = line * factor
    for copy in leaving:
        copy.wait()


def routed(weights, first_moment, second_moment, row_weight, col_weight):
    count = lax.axis_size("dp")
    rows, width = weights.shape
    blocks = width // CHECK_COLS
    vmem = pl.BlockSpec(memory_space=pltpu.VMEM)
    anywhere = pl.BlockSpec(memory_space=pl.ANY)
    tile = jax.ShapeDtypeStruct((count, rows, width), weights.dtype)
    dma = pltpu.SemaphoreType.DMA
    own = pl.pallas_call(
        functools.partial(route, count),
        out_shape=pltpu.VMEM((3, count, rows, width), weights.dtype),
        in_specs=[anywhere] * 3,
        out_specs=vmem,
        scratch_shapes=[
            pltpu.VMEM((3, rows, width), weights.dtype),
            pltpu.VMEM((rows, width), weights.dtype),
            pltpu.VMEM((2, count, rows, width), weights.dtype),
            dma((3,)),
            dma((SPLIT,)),
            dma((SPLIT,)),
            dma((2, 2, SPLIT)),
            dma((3, count, SPLIT)),
            dma((2, count, SPLIT)),
            dma((2, count, SPLIT)),
            dma((2, count, SPLIT)),
            dma((3, count, SPLIT)),
        ],
        compiler_params=pltpu.CompilerParams(
            collective_id=0, has_side_effects=True
        ),
    )(weights, first_moment, second_moment)
    out = pl.pallas_call(
        functools.partial(finish, count),
        out_shape=(tile, tile, tile, jax.ShapeDtypeStruct((3, 1, 1, blocks), jnp.float32)),
        in_specs=[vmem, vmem, vmem],
        out_specs=(anywhere, anywhere, anywhere, vmem),
        scratch_shapes=[pltpu.VMEM((3, 8, width), jnp.float32), dma((3,))],
        compiler_params=pltpu.CompilerParams(vmem_limit_bytes=16 * 1024 * 1024),
    )(own, row_weight, col_weight)
    return tuple(item.reshape(count * rows, width) for item in out[:3]) + (out[3],)


def solution(mesh):
    dp_count, pipe_count, tensor_count = (mesh.shape[a] for a in ("dp", "pipe", "tensor"))
    square = dp_count == tensor_count == 2 * pipe_count and pipe_count == 2
    return jax.shard_map(
        routed if square else shards,
        mesh=mesh,
        in_specs=(
            P(("dp", "pipe", "tensor"), None),
            P(("dp", "pipe", "tensor"), None),
            P(("dp", "pipe", "tensor"), None),
            P(),
            P(),
        ),
        out_specs=(
            P(("pipe", "tensor"), None),
            P(("pipe", "tensor"), None),
            P(("pipe", "tensor"), None),
            P(None, "pipe", "tensor", None),
        ),
        check_vma=False,
    )
```

profile of v0, /device:TPU:5, one launch (start us, length us, event | category | flops | bytes accessed | tf_op | source)
XLA Modules:
  0.0 46.8 jit_solution(1453804159219405623)
XLA Ops:
  0.6 0.0 copy-start.1
  0.6 0.0 copy-start
  0.7 43.8 %shard_map.84.own = bf16[3,4,88,1408]{3,2,1,0:T(8,128)(2,1)S(1)} custom-call(bf16[88,1408]{1,0:T(8,128)(2,1)} %w_ref.1, bf16[88,1408]{1,0:T(8,128)(2,1)} %m_ref.1, bf16[88,1408]{1,0:T(8,128)(2,1)} %v_ref.1), custom_call_target="tpu_custom_call" | custom-call | tf_op jit(solution)/shard_map/pallas_call | solution.py:374
  44.4 0.0 copy-done.1
  44.5 0.0 copy-done
  44.5 2.4 %shard_map.85 = (bf16[4,88,1408]{2,1,0:T(8,128)(2,1)}, bf16[4,88,1408]{2,1,0:T(8,128)(2,1)}, bf16[4,88,1408]{2,1,0:T(8,128)(2,1)}, f32[3,1,1,11]{3,2,1,0:T(1,128)}) custom-call(bf16[3,4,88,1408]{3,2,1,0:T(8,128)(2,1)S(1)} %shard_map.84.own, f32[1408]{0:T(1024)S(1)} %copy-done, f32[1408]{0:T(1024)S(1)} %copy-done.1), custom_call_target="tpu_custom_call" | custom-call | tf_op jit(solution)/shard_map/pallas_call | solution.py:397
Async XLA Ops:
  0.6 43.8 %copy-start.1 = (f32[1408]{0:T(1024)S(1)}, f32[1408]{0:T(1024)}, u32[]{:S(2)}) copy-start(f32[1408]{0:T(1024)} %col_ref.1) | copy-start | bytes 16900
  0.6 43.8 %copy-start = (f32[1408]{0:T(1024)S(1)}, f32[1408]{0:T(1024)}, u32[]{:S(2)}) copy-start(f32[1408]{0:T(1024)} %row_ref.1) | copy-start | bytes 16900
where the time goes:
time: 47 us; the launch traced here: 46.8 us
  Pallas kernels  46.2 us (98%)
  between operations  0.67 us (1%)
    pallas_call x1, Pallas kernels, routed(): pl.pallas_call(functools.partial(route, count), out_shape=pltpu.VMEM((3,...  43.8 us
    pallas_call x1, Pallas kernels, routed(): pl.pallas_call(functools.partial(finish, count), out_shape=(tile, tile, t...  2.38 us

commit v1 on v0

v1 whole, which is shorter than its diff:
```python
import functools

import jax
import jax.numpy as jnp
from jax import lax
from jax.experimental import pallas as pl
from jax.experimental.pallas import tpu as pltpu
from jax.sharding import PartitionSpec as P

CHECK_COLS = 128
SPLIT = 4
OWN_UNITS, OFF_UNITS = 8, 7
ORDER = {
    (True, True, 0): (
        (0, 0, 0), (0, 0, 1), (0, 0, 2), (0, 0, 3), (0, 0, 4), (0, 0, 5), (0, 0, 6), (0, 0, 7),
        (0, 3, 0), (0, 3, 1), (0, 3, 2), (0, 3, 3), (0, 3, 4), (0, 3, 5), (0, 3, 6), (0, 1, 0),
        (0, 3, 7), (0, 2, 0), (0, 1, 1), (0, 2, 1), (0, 1, 2), (0, 2, 2), (0, 1, 3), (0, 2, 3),
        (0, 1, 4), (0, 2, 4), (0, 1, 5), (0, 2, 5), (0, 1, 6), (0, 2, 6), (0, 1, 7), (0, 2, 7),
    ),
    (True, True, 1): (
        (0, 1, 0), (0, 1, 1), (0, 1, 2), (0, 1, 3), (0, 0, 0), (0, 1, 4), (0, 0, 1), (0, 3, 0),
        (0, 1, 5), (0, 0, 2), (0, 3, 1), (0, 1, 6), (0, 0, 3), (0, 3, 2), (0, 0, 4), (0, 3, 3),
        (0, 0, 5), (0, 3, 4), (0, 0, 6), (0, 3, 5), (0, 3, 6), (0, 2, 0), (0, 2, 1), (0, 2, 2),
        (0, 2, 3), (0, 2, 4), (0, 2, 5), (0, 2, 6),
    ),
    (True, True, 2): (
        (0, 2, 0), (0, 2, 1), (0, 2, 2), (0, 2, 3), (0, 2, 4), (0, 2, 5), (0, 2, 6), (0, 2, 7),
        (0, 0, 0), (0, 0, 1), (0, 0, 2), (0, 0, 3), (0, 0, 4), (0, 0, 5), (0, 0, 6), (0, 1, 0),
        (0, 0, 7), (0, 3, 0), (0, 1, 1), (0, 3, 1), (0, 1, 2), (0, 3, 2), (0, 1, 3), (0, 3, 3),
        (0, 1, 4), (0, 3, 4), (0, 1, 5), (0, 3, 5), (0, 1, 6), (0, 3, 6), (0, 1, 7), (0, 3, 7),
    ),
    (True, True, 3): (
        (0, 3, 0), (0, 3, 1), (0, 2, 0), (0, 3, 2), (0, 2, 1), (0, 3, 3), (0, 3, 4), (0, 2, 2),
        (0, 3, 5), (0, 0, 0), (0, 2, 3), (0, 3, 6), (0, 0, 1), (0, 2, 4), (0, 0, 2), (0, 2, 5),
        (0, 0, 3), (0, 2, 6), (0, 0, 4), (0, 0, 5), (0, 0, 6), (0, 1, 0), (0, 1, 1), (0, 1, 2),
        (0, 1, 3), (0, 1, 4), (0, 1, 5), (0, 1, 6),
    ),
    (True, False, 0): (
        (1, 0, 0), (1, 1, 0), (1, 0, 1), (1, 1, 1), (1, 0, 2), (1, 1, 2), (1, 0, 3), (1, 1, 3),
        (1, 0, 4), (1, 1, 4), (1, 0, 5), (1, 1, 5), (1, 0, 6), (1, 1, 6), (0, 1, 8), (0, 3, 8),
        (0, 1, 9), (0, 3, 9), (0, 1, 10), (0, 3, 10), (0, 1, 11), (0, 3, 11), (0, 0, 8), (0, 0, 9),
        (0, 0, 10), (0, 2, 8), (0, 0, 11), (0, 2, 9), (0, 2, 10), (0, 2, 11),
    ),
    (True, False, 1): (
        (1, 1, 0), (1, 1, 1), (1, 1, 2), (1, 1, 3), (1, 1, 4), (1, 1, 5), (1, 1, 6), (0, 1, 7),
        (0, 1, 8), (0, 1, 9), (0, 1, 10), (0, 1, 11), (0, 3, 7), (0, 3, 8), (0, 3, 9), (0, 3, 10),
        (0, 0, 7), (0, 3, 11), (0, 2, 7), (0, 0, 8), (0, 0, 9), (0, 2, 8), (0, 0, 10), (0, 0, 11),
        (0, 2, 9), (0, 2, 10), (0, 2, 11),
    ),
    (True, False, 2): (
        (1, 0, 0), (1, 1, 0), (1, 0, 1), (1, 1, 1), (1, 0, 2), (1, 1, 2), (1, 0, 3), (1, 1, 3),
        (1, 0, 4), (1, 1, 4), (1, 0, 5), (1, 1, 5), (1, 0, 6), (1, 1, 6), (0, 3, 8), (0, 3, 9),
        (0, 1, 8), (0, 3, 10), (0, 1, 9), (0, 1, 10), (0, 3, 11), (0, 1, 11), (0, 2, 8), (0, 2, 9),
        (0, 2, 10), (0, 0, 8), (0, 2, 11), (0, 0, 9), (0, 0, 10), (0, 0, 11),
    ),
    (True, False, 3): (
        (1, 0, 0), (1, 0, 1), (1, 0, 2), (1, 0, 3), (1, 0, 4), (1, 0, 5), (1, 0, 6), (0, 3, 7),
        (0, 3, 8), (0, 3, 9), (0, 3, 10), (0, 3, 11), (0, 0, 7), (0, 0, 8), (0, 0, 9), (0, 0, 10),
        (0, 1, 7), (0, 0, 11), (0, 1, 8), (0, 1, 9), (0, 1, 10), (0, 2, 7), (0, 1, 11), (0, 2, 8),
        (0, 2, 9), (0, 2, 10), (0, 2, 11),
    ),
    (False, True, 0): (
        (0, 1, 8), (0, 3, 8), (0, 1, 9), (0, 3, 9), (0, 1, 10), (0, 3, 10), (0, 1, 11), (0, 3, 11),
        (0, 0, 8), (0, 0, 9), (0, 0, 10), (0, 2, 8), (0, 0, 11), (0, 2, 9), (0, 2, 10), (0, 2, 11),
    ),
    (False, True, 1): (
        (0, 1, 7), (0, 1, 8), (0, 1, 9), (0, 1, 10), (0, 1, 11), (0, 3, 7), (0, 3, 8), (0, 3, 9),
        (0, 3, 10), (0, 0, 7), (0, 3, 11), (0, 0, 8), (0, 2, 7), (0, 0, 9), (0, 0, 10), (0, 2, 8),
        (0, 0, 11), (0, 2, 9), (0, 2, 10), (0, 2, 11),
    ),
    (False, True, 2): (
        (0, 3, 8), (0, 3, 9), (0, 1, 8), (0, 3, 10), (0, 1, 9), (0, 1, 10), (0, 3, 11), (0, 1, 11),
        (0, 2, 8), (0, 2, 9), (0, 2, 10), (0, 0, 8), (0, 2, 11), (0, 0, 9), (0, 0, 10), (0, 0, 11),
    ),
    (False, True, 3): (
        (0, 3, 7), (0, 3, 8), (0, 3, 9), (0, 3, 10), (0, 3, 11), (0, 0, 7), (0, 0, 8), (0, 0, 9),
        (0, 0, 10), (0, 1, 7), (0, 0, 11), (0, 1, 8), (0, 1, 9), (0, 1, 10), (0, 2, 7), (0, 1, 11),
        (0, 2, 8), (0, 2, 9), (0, 2, 10), (0, 2, 11),
    ),
    (False, False, 0): (
        (1, 1, 8), (1, 1, 9), (1, 1, 10), (1, 1, 11), (0, 0, 7), (0, 0, 8), (0, 0, 9), (0, 0, 0),
        (0, 0, 10), (0, 0, 11), (0, 0, 1), (0, 3, 7), (0, 1, 0), (0, 3, 8), (0, 0, 2), (0, 3, 9),
        (0, 1, 1), (0, 3, 10), (0, 0, 3), (0, 2, 7), (0, 3, 11), (0, 1, 2), (0, 2, 8), (0, 0, 4),
        (0, 2, 9), (0, 3, 0), (0, 2, 10), (0, 1, 3), (0, 1, 7), (0, 0, 5), (0, 2, 11), (0, 3, 1),
        (0, 1, 8), (0, 1, 4), (0, 1, 9), (0, 0, 6), (0, 1, 10), (0, 3, 2), (0, 1, 11), (0, 1, 5),
        (0, 3, 3), (0, 1, 6), (0, 3, 4), (0, 3, 5), (0, 3, 6), (0, 2, 0), (0, 2, 1), (0, 2, 2),
        (0, 2, 3), (0, 2, 4), (0, 2, 5), (0, 2, 6),
    ),
    (False, False, 1): (
        (1, 0, 8), (1, 1, 8), (1, 0, 9), (1, 1, 9), (1, 0, 10), (1, 1, 10), (1, 0, 11), (1, 1, 11),
        (0, 1, 0), (0, 1, 1), (0, 1, 2), (0, 1, 3), (0, 1, 4), (0, 1, 5), (0, 1, 6), (0, 1, 7),
        (0, 3, 0), (0, 0, 8), (0, 3, 1), (0, 3, 2), (0, 0, 9), (0, 3, 3), (0, 3, 4), (0, 0, 10),
        (0, 3, 5), (0, 2, 8), (0, 3, 6), (0, 2, 9), (0, 3, 7), (0, 0, 11), (0, 0, 0), (0, 2, 10),
        (0, 2, 0), (0, 2, 11), (0, 0, 1), (0, 2, 1), (0, 0, 2), (0, 2, 2), (0, 0, 3), (0, 2, 3),
        (0, 0, 4), (0, 1, 8), (0, 2, 4), (0, 0, 5), (0, 1, 9), (0, 2, 5), (0, 0, 6), (0, 1, 10),
        (0, 2, 6), (0, 3, 8), (0, 0, 7), (0, 1, 11), (0, 2, 7), (0, 3, 9), (0, 3, 10), (0, 3, 11),
    ),
    (False, False, 2): (
        (1, 0, 8), (1, 0, 9), (1, 0, 10), (1, 0, 11), (0, 2, 7), (0, 2, 8), (0, 2, 9), (0, 2, 0),
        (0, 2, 10), (0, 2, 11), (0, 2, 1), (0, 0, 7), (0, 0, 8), (0, 2, 2), (0, 0, 9), (0, 0, 10),
        (0, 2, 3), (0, 1, 7), (0, 3, 7), (0, 3, 0), (0, 0, 11), (0, 2, 4), (0, 3, 8), (0, 0, 0),
        (0, 1, 8), (0, 3, 1), (0, 3, 9), (0, 2, 5), (0, 3, 10), (0, 0, 1), (0, 1, 9), (0, 3, 2),
        (0, 3, 11), (0, 2, 6), (0, 1, 10), (0, 0, 2), (0, 1, 11), (0, 3, 3), (0, 0, 3), (0, 3, 4),
        (0, 0, 4), (0, 3, 5), (0, 0, 5), (0, 3, 6), (0, 0, 6), (0, 1, 0), (0, 1, 1), (0, 1, 2),
        (0, 1, 3), (0, 1, 4), (0, 1, 5), (0, 1, 6),
    ),
    (False, False, 3): (
        (1, 0, 8), (1, 1, 8), (1, 0, 9), (1, 1, 9), (1, 0, 10), (1, 1, 10), (1, 0, 11), (1, 1, 11),
        (0, 3, 0), (0, 3, 1), (0, 3, 2), (0, 3, 3), (0, 3, 4), (0, 3, 5), (0, 3, 6), (0, 3, 7),
        (0, 0, 0), (0, 2, 8), (0, 0, 1), (0, 0, 2), (0, 2, 9), (0, 0, 3), (0, 0, 8), (0, 0, 4),
        (0, 2, 10), (0, 0, 5), (0, 0, 9), (0, 0, 6), (0, 2, 11), (0, 2, 0), (0, 0, 10), (0, 0, 7),
        (0, 1, 0), (0, 0, 11), (0, 2, 1), (0, 1, 1), (0, 2, 2), (0, 1, 2), (0, 2, 3), (0, 1, 3),
        (0, 2, 4), (0, 3, 8), (0, 1, 4), (0, 2, 5), (0, 3, 9), (0, 1, 5), (0, 2, 6), (0, 3, 10),
        (0, 1, 6), (0, 1, 8), (0, 2, 7), (0, 3, 11), (0, 1, 7), (0, 1, 9), (0, 1, 10), (0, 1, 11),
    ),
}


def for_sending(array):
    return jax.tree.map(lambda a: a.astype(jnp.bfloat16) if a.dtype == jnp.float32 else a, array)


def column_sums(data, row_part, col_weight, col_blocks):
    row_mixed = jnp.dot(
        row_part[None, :], data.astype(jnp.float32), precision=lax.Precision.HIGHEST
    )[0]
    return jnp.sum((row_mixed * col_weight).reshape(col_blocks, -1), axis=1)


def shards(weights, first_moment, second_moment, row_weight, col_weight):
    dp_count = lax.axis_size("dp")
    pipe_count = lax.axis_size("pipe")
    tensor_count = lax.axis_size("tensor")
    shard_rows, width = weights.shape
    dp_section = dp_count // pipe_count
    tile_shards = dp_count // tensor_count
    piece_cols = width // dp_count
    tile_rows = shard_rows * dp_count
    col_blocks = width // CHECK_COLS
    factor = float(tile_rows * CHECK_COLS) ** (-0.5)
    sources = (weights, first_moment, second_moment)
    exchanged = (
        lax.all_to_all(sources[0], "dp", split_axis=1, concat_axis=0, tiled=True),
        lax.all_to_all(sources[1], "dp", split_axis=1, concat_axis=0, tiled=True),
        lax.all_to_all(sources[2], "dp", split_axis=1, concat_axis=0, tiled=True),
    )
    grouped = tuple(
        (item.reshape(pipe_count, dp_section, shard_rows, piece_cols) for item in exchanged)
    )
    sectioned = jax.tree.map(
        lambda part, own: part.astype(own.dtype),
        lax.all_to_all(for_sending(grouped), "pipe", split_axis=0, concat_axis=2, tiled=True),
        grouped,
    )
    routed = tuple(
        (item.reshape(tensor_count, tile_shards, 1, shard_rows, piece_cols) for item in sectioned)
    )
    arrived = jax.tree.map(
        lambda part, own: part.astype(own.dtype),
        lax.all_to_all(for_sending(routed), "tensor", split_axis=0, concat_axis=2, tiled=True),
        routed,
    )
    flat_pieces = tuple((item.reshape(tile_rows, piece_cols) for item in arrived))
    tiles = jax.tree.map(
        lambda part, own: part.astype(own.dtype),
        lax.all_gather(for_sending(flat_pieces), "dp", axis=1, tiled=True),
        flat_pieces,
    )
    tensor_pos = lax.axis_index("tensor")
    flat_index = (
        lax.axis_index("dp") * pipe_count + lax.axis_index("pipe")
    ) * tensor_count + tensor_pos
    in_section = flat_index % (dp_count * tensor_count)
    section_of = flat_index // (dp_count * tensor_count)
    tile_of = in_section // dp_count
    row_part = lax.dynamic_slice_in_dim(row_weight, in_section * shard_rows, shard_rows)
    partial_value = jnp.stack(
        [column_sums(item, row_part, col_weight, col_blocks) for item in sources]
    )
    section_hit = (jnp.arange(pipe_count) == section_of).astype(jnp.float32)
    tile_hit = (jnp.arange(tensor_count) == tile_of).astype(jnp.float32)
    spread = (
        partial_value[:, None, None, :]
        * section_hit[None, :, None, None]
        * tile_hit[None, None, :, None]
    )
    summed = lax.psum(spread, ("dp", "pipe", "tensor"))
    checks = (
        lax.dynamic_slice(summed, (0, lax.axis_index("pipe"), tensor_pos, 0), (3, 1, 1, col_blocks))
        * factor
    )
    return (tiles[0], tiles[1], tiles[2], checks)


def remote(src, dst, send_sem, recv_sem, where):
    return pltpu.make_async_remote_copy(
        src_ref=src,
        dst_ref=dst,
        send_sem=send_sem,
        recv_sem=recv_sem,
        device_id=where,
        device_id_type=pl.DeviceIdType.MESH,
    )


def route(
    count,
    w_ref,
    m_ref,
    v_ref,
    own,
    src,
    crossed,
    transit,
    load_sem,
    cross_send,
    cross_recv,
    z_send,
    relay_send,
    own_recv,
    transit_recv,
    hop_send,
    core_send,
):
    dp, y, z = lax.axis_index("dp"), lax.axis_index("pipe"), lax.axis_index("tensor")
    x, core = dp // 2, dp % 2
    hub = z // 2
    diag = x == y
    mine = 2 * core + y
    rows = w_ref.shape[0]
    edges = [rows // 8 * h // SPLIT * 8 for h in range(SPLIT)] + [rows]
    cuts = [pl.ds(low, high - low) for low, high in zip(edges, edges[1:])]
    units = range(3 * SPLIT)

    def unit(ref, u):
        return ref.at[u // SPLIT, cuts[u % SPLIT]]

    def at(to_x, to_y, to_core, to_z=None):
        return {"dp": to_x * 2 + to_core, "pipe": to_y, "tensor": z if to_z is None else to_z}

    core_to = at(x, y, 1 - core)
    x_to = at(1 - x, y, 1 - core)
    y_to = at(x, 1 - y, 1 - core)
    both_to = at(1 - x, 1 - y, 1 - core)

    ins = (w_ref, m_ref, v_ref)
    loads = [pltpu.make_async_copy(ins[a], src.at[a], load_sem.at[a]) for a in range(3)]
    for load in loads:
        load.start()

    barrier = pltpu.get_barrier_semaphore()
    partners = [core_to, x_to, y_to, both_to, at(x, 1 - y, core)]
    for step in range(1, count):
        partners += [at(x, y, c, (z + step) % count) for c in (core, 1 - core)]
    for where in partners:
        pl.semaphore_signal(barrier, inc=1, device_id=where, device_id_type=pl.DeviceIdType.MESH)
    pl.semaphore_wait(barrier, len(partners))
    for load in loads:
        load.wait()

    def start(copy):
        copy.start()

    def sent(copy):
        copy.wait_send()

    def home(on_diag, k, u):
        if on_diag:
            return unit(own.at[k], u), own_recv.at[k, u]
        return unit(transit.at[k], u), transit_recv.at[k, u]

    def cross(on_diag, u, act):
        slot, sem = home(not on_diag, z, u)
        relay = unit(crossed.at[core], u)

        @pl.when(mine == z)
        def _():
            act(remote(unit(src, u), slot, cross_send.at[u], sem, at(x, 1 - y, hub)))

        @pl.when(mine != z)
        def _():
            act(remote(unit(src, u), relay, cross_send.at[u], cross_recv.at[core, u], at(x, 1 - y, 1 - hub)))

    def along(on_diag, u, act):
        slot, sem = home(on_diag, z, u)

        @pl.when(mine != z)
        def _():
            act(remote(unit(src, u), slot, z_send.at[u], sem, at(x, y, core, mine)))

        if act is start:

            @pl.when(mine == z)
            def _():
                pltpu.make_async_copy(unit(src, u), slot, sem).start()

    def relay(on_diag, c, u):
        slot, sem = home(on_diag, z, u)
        return remote(unit(crossed.at[c], u), slot, relay_send.at[c, u], sem, at(x, y, c, 2 * c + 1 - y))

    def landed(slot, sem):
        pltpu.make_async_copy(slot, slot, sem).wait()

    def arrive(k, u):
        landed(*home(True, k, u))

    def across(k, u):
        slot, sem = home(True, k, u)
        return remote(slot, slot, core_send.at[k, u], sem, core_to)

    def forward_x(k, u):
        slot, sem = home(True, k, u)
        return remote(slot, slot, hop_send.at[0, k, u], sem, x_to)

    def forward_off(n, k, u):
        slot, sem = home(True, k, u)
        return remote(unit(transit.at[k], u), slot, hop_send.at[n, k, u], sem, (y_to, both_to)[n])

    def flip(low, high):
        return low + x * (high - 2 * low)

    for on_diag in (True, False):

        @pl.when(diag == on_diag)
        def _():
            limit = OWN_UNITS if on_diag else OFF_UNITS
            for u in units:
                if (u < limit) != on_diag:
                    cross(on_diag, u, start)
            for u in units:
                if (u < limit) == on_diag:
                    along(on_diag, u, start)

    place = flip(z, count - 1)

    def run(on_diag, is_hub, zr):
        limit = OFF_UNITS if zr % 2 else OWN_UNITS
        for kind, kr, u in ORDER[on_diag, is_hub, zr]:
            if kind:
                c = flip(kr, 1)
                landed(unit(crossed.at[c], u), cross_recv.at[c, u])
                relay(on_diag, c, u).start()
                continue
            k = flip(kr, count - 1)
            if is_hub and not on_diag:
                landed(*home(False, k, u))
                forward_off(0, k, u).start()
                forward_off(1, k, u).start()
            else:
                arrive(k, u)
                if is_hub:
                    forward_x(k, u).start()
                across(k, u).start()

        @pl.loop(0, count)
        def _(kr):
            k = flip(kr, count - 1)
            for u in units:
                here = is_hub == (on_diag and u < limit)
                if is_hub and not on_diag:
                    arrive(k, u)
                    if u >= limit:
                        forward_off(0, k, u).wait_send()
                        forward_off(1, k, u).wait_send()
                elif here:
                    if is_hub:
                        forward_x(k, u).wait_send()
                    across(k, u).wait_send()
                else:
                    arrive(k, u)

        if not is_hub:
            for cr in (0, 1):
                for u in units:
                    odd = OFF_UNITS if on_diag else OWN_UNITS
                    if 2 * cr + on_diag != zr and (u < odd) == on_diag:
                        relay(on_diag, flip(cr, 1), u).wait_send()

    for on_diag in (True, False):
        for is_hub in (True, False):
            for zr in range(count):

                @pl.when((diag == on_diag) & ((hub == core) == is_hub) & (place == zr))
                def _():
                    run(on_diag, is_hub, zr)

    for on_diag in (True, False):

        @pl.when(diag == on_diag)
        def _():
            limit = OWN_UNITS if on_diag else OFF_UNITS
            for u in units:
                if (u < limit) == on_diag:
                    along(on_diag, u, sent)
                else:
                    cross(on_diag, u, sent)


def finish(count, own, row_ref, col_ref, out0, out1, out2, check_ref, acc, out_sem):
    rows, width = own.shape[2:]
    outs = (out0, out1, out2)
    leaving = [
        pltpu.make_async_copy(own.at[k, a], outs[a].at[k], out_sem.at[a, k])
        for a in range(3)
        for k in range(count)
    ]
    for copy in leaving:
        copy.start()
    acc[...] = jnp.zeros_like(acc)
    for k in range(count):
        first = (lax.axis_index("tensor") * count + k) * rows
        everyone = jnp.broadcast_to(row_ref[...].reshape(1, width), (8, width))
        part = pltpu.roll(everyone, (width - first) % width, 1)[:, :rows]
        high = part.astype(jnp.bfloat16).astype(jnp.float32)
        middle = (part - high).astype(jnp.bfloat16).astype(jnp.float32)
        low = part - high - middle
        line = lax.broadcasted_iota(jnp.int32, (8, rows), 0)
        terms = jnp.where(
            line == 0, high, jnp.where(line == 1, middle, jnp.where(line == 2, low, 0.0))
        )
        terms = terms.astype(jnp.bfloat16)
        for a in range(3):
            acc[a] += jnp.dot(terms, own[k, a], preferred_element_type=jnp.float32)

    factor = float(rows * count * CHECK_COLS) ** (-0.5)
    blocks = width // CHECK_COLS
    weight = col_ref[...].reshape(1, width)
    for a in range(3):
        mixed = jnp.sum(acc[a], axis=0, keepdims=True) * weight
        lane = lax.broadcasted_iota(jnp.int32, (1, blocks), 1)
        line = jnp.zeros((1, blocks), jnp.float32)
        for e in range(blocks):
            part = jnp.sum(mixed[:, e * CHECK_COLS : (e + 1) * CHECK_COLS], axis=1, keepdims=True)
            line = jnp.where(lane == e, part, line)
        check_ref[a, 0] = line * factor
    for copy in leaving:
        copy.wait()


def routed(weights, first_moment, second_moment, row_weight, col_weight):
    count = lax.axis_size("dp")
    rows, width = weights.shape
    blocks = width // CHECK_COLS
    vmem = pl.BlockSpec(memory_space=pltpu.VMEM)
    anywhere = pl.BlockSpec(memory_space=pl.ANY)
    tile = jax.ShapeDtypeStruct((count, rows, width), weights.dtype)
    dma = pltpu.SemaphoreType.DMA
    own = pl.pallas_call(
        functools.partial(route, count),
        out_shape=pltpu.VMEM((count, 3, rows, width), weights.dtype),
        in_specs=[anywhere] * 3,
        out_specs=vmem,
        scratch_shapes=[
            pltpu.VMEM((3, rows, width), weights.dtype),
            pltpu.VMEM((2, 3, rows, width), weights.dtype),
            pltpu.VMEM((count, 3, rows, width), weights.dtype),
            dma((3,)),
            dma((3 * SPLIT,)),
            dma((2, 3 * SPLIT)),
            dma((3 * SPLIT,)),
            dma((2, 3 * SPLIT)),
            dma((count, 3 * SPLIT)),
            dma((count, 3 * SPLIT)),
            dma((2, count, 3 * SPLIT)),
            dma((count, 3 * SPLIT)),
        ],
        compiler_params=pltpu.CompilerParams(
            collective_id=0, has_side_effects=True
        ),
    )(weights, first_moment, second_moment)
    out = pl.pallas_call(
        functools.partial(finish, count),
        out_shape=(tile, tile, tile, jax.ShapeDtypeStruct((3, 1, 1, blocks), jnp.float32)),
        in_specs=[vmem, vmem, vmem],
        out_specs=(anywhere, anywhere, anywhere, vmem),
        scratch_shapes=[pltpu.VMEM((3, 8, width), jnp.float32), dma((3, count))],
        compiler_params=pltpu.CompilerParams(vmem_limit_bytes=16 * 1024 * 1024),
    )(own, row_weight, col_weight)
    return tuple(item.reshape(count * rows, width) for item in out[:3]) + (out[3],)


def solution(mesh):
    dp_count, pipe_count, tensor_count = (mesh.shape[a] for a in ("dp", "pipe", "tensor"))
    square = dp_count == tensor_count == 2 * pipe_count and pipe_count == 2
    return jax.shard_map(
        routed if square else shards,
        mesh=mesh,
        in_specs=(
            P(("dp", "pipe", "tensor"), None),
            P(("dp", "pipe", "tensor"), None),
            P(("dp", "pipe", "tensor"), None),
            P(),
            P(),
        ),
        out_specs=(
            P(("pipe", "tensor"), None),
            P(("pipe", "tensor"), None),
            P(("pipe", "tensor"), None),
            P(None, "pipe", "tensor", None),
        ),
        check_vma=False,
    )
```

time: 47 us -> 40.6 us (0.86)
  the two profiles are of different devices: /device:TPU:5 before, /device:TPU:11 now
where the time goes in v1:
time: 40.6 us; the launch traced here: 40.4 us
  Pallas kernels  39.8 us (98%)
  between operations  0.67 us (2%)
    pallas_call x1, Pallas kernels, routed(): pl.pallas_call(functools.partial(route, count), out_shape=pltpu.VMEM((cou...  37.2 us
    pallas_call x1, Pallas kernels, routed(): pl.pallas_call(functools.partial(finish, count), out_shape=(tile, tile, t...  2.59 us

profile of v1, /device:TPU:11, one launch (start us, length us, event | category | flops | bytes accessed | tf_op | source)
XLA Modules:
  0.0 40.4 jit_solution(10626261057631379285)
XLA Ops:
  0.6 0.0 copy-start.1
  0.6 0.0 copy-start
  0.7 37.2 %shard_map.84.own = bf16[4,3,88,1408]{3,2,1,0:T(8,128)(2,1)S(1)} custom-call(bf16[88,1408]{1,0:T(8,128)(2,1)} %w_ref.1, bf16[88,1408]{1,0:T(8,128)(2,1)} %m_ref.1, bf16[88,1408]{1,0:T(8,128)(2,1)} %v_ref.1), custom_call_target="tpu_custom_call" | custom-call | tf_op jit(solution)/shard_map/pallas_call | solution.py:448
  37.8 0.0 copy-done.1
  37.8 0.0 copy-done
  37.9 2.6 %shard_map.85 = (bf16[4,88,1408]{2,1,0:T(8,128)(2,1)}, bf16[4,88,1408]{2,1,0:T(8,128)(2,1)}, bf16[4,88,1408]{2,1,0:T(8,128)(2,1)}, f32[3,1,1,11]{3,2,1,0:T(1,128)}) custom-call(bf16[4,3,88,1408]{3,2,1,0:T(8,128)(2,1)S(1)} %shard_map.84.own, f32[1408]{0:T(1024)S(1)} %copy-done, f32[1408]{0:T(1024)S(1)} %copy-done.1), custom_call_target="tpu_custom_call" | custom-call | tf_op jit(solution)/shard_map/pallas_call | solution.py:471
Async XLA Ops:
  0.6 37.2 %copy-start.1 = (f32[1408]{0:T(1024)S(1)}, f32[1408]{0:T(1024)}, u32[]{:S(2)}) copy-start(f32[1408]{0:T(1024)} %col_ref.1) | copy-start | bytes 16900
  0.6 37.2 %copy-start = (f32[1408]{0:T(1024)S(1)}, f32[1408]{0:T(1024)}, u32[]{:S(2)}) copy-start(f32[1408]{0:T(1024)} %row_ref.1) | copy-start | bytes 16900
